TPU v7x, 32 devices: a whole 2x2x4 slice. The times are simulated.
32 devices in a mesh: rows: 8 (over z, x), grp: 4 (over y, core).
Axes of the slice: x: 2, y: 2, z: 4, core: 2. Of those that a mesh axis runs over, the one named last changes fastest.
Arguments:
- sketch: float32 [2048, 8192], P(None, ('rows', 'grp')), may hold values from -0.125 to 0.125
- prior_basis: float32 [8192, 512], P(('rows', 'grp'))
- panel_block: float32 [8192, 256], P(('rows', 'grp'))
- panel_index: int32 [1], replicated, may hold values from 0 to 2
- prior_count: int32 [1], replicated, may hold values from 384 to 512
Outputs:
- new_basis: float32 [8192, 128], P(('rows', 'grp'))
- factors: float32 [640, 128], replicated
All inputs are finite; a program needn't handle non-finite values.
Results may differ from a plain program's by a relative error of at most 0.00011.
Values sent between devices are 32-bit elements; how exact they have to be, the bound alone decides.
A program may use at most 64 MiB of HBM per device.

v0:
```python
import jax
import jax.numpy as jnp
from jax import lax
from jax.sharding import PartitionSpec as P

P_SIZE = 64


def matmul(left, right):
    return jnp.dot(left, right, precision=lax.Precision.HIGHEST)


def right_solve(factor, values):
    return jax.scipy.linalg.solve_triangular(factor, values.T, lower=True).T


def shards(sketch, prior_basis, panel_block, panel_index, prior_count):
    width = prior_basis.shape[1]
    column_keep = (jnp.arange(width) < prior_count[0]).astype(jnp.float32)
    masked = prior_basis * column_keep
    start = panel_index[0] * P_SIZE
    chosen = lax.dynamic_slice_in_dim(panel_block, start, 2 * P_SIZE, 1)
    first = chosen[:, :P_SIZE]
    second = chosen[:, P_SIZE:]
    local_prior = matmul(sketch, masked)
    local_panels = matmul(sketch, chosen)
    prior_sketch = lax.psum(local_prior, ("rows", "grp"))
    sketch_one = lax.psum(local_panels[:, :P_SIZE], ("rows", "grp"))
    sketch_two = lax.psum(local_panels[:, P_SIZE:], ("rows", "grp"))
    gram_prior = matmul(prior_sketch.T, prior_sketch) + jnp.diag(1.0 - column_keep)
    prior_factor = jnp.linalg.cholesky(gram_prior)
    coef_one = jax.scipy.linalg.cho_solve((prior_factor, True), matmul(prior_sketch.T, sketch_one))
    skres_one = sketch_one - matmul(prior_sketch, coef_one)
    coef_two = jax.scipy.linalg.cho_solve((prior_factor, True), matmul(prior_sketch.T, sketch_two))
    skres_two = sketch_two - matmul(prior_sketch, coef_two)
    resid_one = first - matmul(masked, coef_one)
    gram_first = lax.psum(matmul(resid_one.T, resid_one), ("rows", "grp"))
    tri_one = jnp.linalg.cholesky(gram_first)
    basis_one = right_solve(tri_one, resid_one)
    skbasis_one = right_solve(tri_one, skres_one)
    resid_two = second - matmul(masked, coef_two)
    small_gram = matmul(skbasis_one.T, skbasis_one)
    small_cross = matmul(skbasis_one.T, skres_two)
    small_factor = jnp.linalg.cholesky(small_gram)
    inner = jax.scipy.linalg.cho_solve((small_factor, True), small_cross)
    final_two = resid_two - matmul(basis_one, inner)
    gram_second = lax.psum(matmul(final_two.T, final_two), ("rows", "grp"))
    tri_two = jnp.linalg.cholesky(gram_second)
    basis_two = right_solve(tri_two, final_two)
    total_rows = prior_basis.shape[0] * lax.axis_size("rows") * lax.axis_size("grp")
    scale_rows = jnp.sqrt(jnp.float32(total_rows))
    new_basis = jnp.concatenate([basis_one, basis_two], axis=1) * scale_rows
    upper = jnp.concatenate([tri_one.T, inner], axis=1)
    lower_rows = jnp.concatenate([jnp.zeros((P_SIZE, P_SIZE), jnp.float32), tri_two.T], axis=1)
    factors = jnp.concatenate(
        [jnp.concatenate([coef_one, coef_two], axis=1), upper, lower_rows], axis=0
    )
    return (new_basis, factors)


def solution(mesh):
    placed = (
        P(None, ("rows", "grp")),
        P(("rows", "grp"), None),
        P(("rows", "grp"), None),
        P(),
        P(),
    )
    return jax.shard_map(
        shards,
        mesh=mesh,
        in_specs=placed,
        out_specs=(P(("rows", "grp"), None), P()),
        check_vma=False,
    )
```

profile of v0, /device:TPU:0, one launch (start us, length us, event | category | flops | bytes accessed | tf_op | source)
XLA Modules:
  0.0 491.8 jit_solution(1554851804183788715)
XLA Ops:
  8.8 3.3 convolution_bitcast_fusion.1
  13.8 8.3 %convolution_bitcast_fusion = f32[2048,512]{0,1:T(8,128)} fusion(f32[2048,256]{1,0:T(8,128)S(1)} %copy-done, f32[256,512]{1,0:T(8,128)S(1)} %copy-done.6, f32[512]{0:T(512)S(1)} %fusion.100), kind=kOutput, calls=%fused_computation.2 | convolution fusion | flops 3221356544 | bytes 6817792 | tf_op jit(solution)/shard_map/dot_general | solution.py:10
  24.6 148.8 %all-reduce.5.cloned.1.call-done = (f32[2048,512]{0,1:T(8,128)}, f32[2048,64]{0,1:T(8,128)}, f32[2048,64]{0,1:T(8,128)}) async-done(((f32[2048,512]{0,1:T(8,128)}, f32[2048,64]{0,1:T(8,128)}, f32[2048,64]{0,1:T(8,128)}), (f32[2048,512]{0,1:T(8,128)}, f32[2048,64]{0,1:T(8,128)}, f32[2048,64]{0,1:T(8,128)})) %all-reduce.5.cloned.1.call-update) | async-done | bytes 5242896 | tf_op jit(solution)/shard_map/psum | solution.py:27
  173.4 9.5 %fusion.116 = f32[512,512]{1,0:T(8,128)S(1)} fusion(f32[2048,512]{0,1:T(8,128)} %get-tuple-element.31), kind=kOutput, calls=%fused_computation.194 | convolution fusion | flops 6442450944 | bytes 5242880 | tf_op jit(solution)/shard_map/dot_general | solution.py:10
  186.7 11.7 %cholesky.119 = f32[128,128]{1,0:T(8,128)S(1)} custom-call(f32[128,128]{1,0:T(8,128)S(1)} %cholesky.353), custom_call_target="Cholesky" | custom-call | tf_op jit(solution)/shard_map/jit(cholesky)/cholesky | solution.py:31
  198.4 9.8 %custom-call.48 = f32[1,128,128]{1,2,0:T(8,128)S(1)} custom-call(f32[1,128,128]{2,1,0:T(8,128)S(1)} %get-tuple-element.49), custom_call_target="InvertDiagBlocksLowerTriangular" | custom-call | tf_op jit(solution)/shard_map/jit(cholesky)/cholesky | solution.py:31
  210.9 11.7 %cholesky.242 = f32[128,128]{1,0:T(8,128)S(1)} custom-call(f32[128,128]{1,0:T(8,128)S(1)} %cholesky.357), custom_call_target="Cholesky" | custom-call | tf_op jit(solution)/shard_map/jit(cholesky)/cholesky | solution.py:31
  222.6 10.2 %custom-call.49 = f32[1,128,128]{1,2,0:T(8,128)S(1)} custom-call(f32[1,128,128]{2,1,0:T(8,128)S(1)} %get-tuple-element.46), custom_call_target="InvertDiagBlocksLowerTriangular" | custom-call | tf_op jit(solution)/shard_map/jit(cholesky)/cholesky | solution.py:31
  234.4 11.7 %cholesky.263 = f32[128,128]{1,0:T(8,128)S(1)} custom-call(f32[128,128]{1,0:T(8,128)S(1)} %cholesky.362), custom_call_target="Cholesky" | custom-call | tf_op jit(solution)/shard_map/jit(cholesky)/cholesky | solution.py:31
  246.8 9.8 %custom-call.50 = f32[1,128,128]{1,2,0:T(8,128)S(1)} custom-call(f32[1,128,128]{2,1,0:T(8,128)S(1)} %get-tuple-element.43), custom_call_target="InvertDiagBlocksLowerTriangular" | custom-call | tf_op jit(solution)/shard_map/jit(cholesky)/cholesky | solution.py:31
  258.1 11.7 %cholesky.280 = f32[128,128]{1,0:T(8,128)S(1)} custom-call(f32[128,128]{1,0:T(8,128)S(1)} %convolution_subtract_fusion.7), custom_call_target="Cholesky" | custom-call | tf_op jit(solution)/shard_map/jit(cholesky)/cholesky | solution.py:31
  274.0 1.5 select_select_fusion
  275.6 10.8 %while.4 = (s32[]{:T(128)}, f32[512,512]{1,0:T(8,128)S(1)}, s32[4,2]{0,1:T(2,128)S(1)}, f32[4,128,128]{2,1,0:T(8,128)}, s32[]{:T(128)}) while((s32[]{:T(128)}, f32[512,512]{1,0:T(8,128)S(1)}, s32[4,2]{0,1:T(2,128)S(1)}, f32[4,128,128]{2,1,0:T(8,128)}, s32[]{:T(128)}) %tuple.43), condition=%wide.while_cond, body=%wide.while_body.sunk | while | flops 2 | bytes 132705 | solution.py:32
  276.3 2.0 bitcast_dynamic-update-slice_fusion.2
  278.9 2.0 bitcast_dynamic-update-slice_fusion.2
  281.6 2.0 bitcast_dynamic-update-slice_fusion.2
  284.3 2.0 bitcast_dynamic-update-slice_fusion.2
  286.3 40.2 %custom-call.55 = f32[4,128,128]{1,2,0:T(8,128)S(1)} custom-call(f32[4,128,128]{2,1,0:T(8,128)} %get-tuple-element.19), custom_call_target="InvertDiagBlocksLowerTriangular" | custom-call | tf_op jit(solution)/shard_map/jit(_cho_solve)/triangular_solve | solution.py:32
  326.5 6.6 %fusion.117 = f32[512,64]{0,1:T(8,128)S(1)} fusion(f32[2048,512]{0,1:T(8,128)} %get-tuple-element.31, f32[2048,64]{0,1:T(8,128)} %get-tuple-element.33), kind=kOutput, calls=%fused_computation.195 | convolution fusion | flops 805306368 | bytes 4849664 | tf_op jit(solution)/shard_map/dot_general | solution.py:10
  336.7 3.7 convolution_subtract_fusion.1
  341.8 39.2 %psum.37 = f32[64,64]{0,1:T(8,128)S(1)} all-reduce(f32[64,64]{0,1:T(8,128)S(1)} %fusion.118), channel_id=1, replica_groups=mesh['rows'=8,'grp'=4] {'rows','grp'}, use_global_device_ids=true, to_apply=%region_10.12 | all-reduce | flops 4096 | bytes 32768 | tf_op jit(solution)/shard_map/psum | solution.py:37
  381.1 5.8 %cholesky.322 = f32[64,64]{1,0:T(8,128)S(1)} custom-call(f32[64,64]{1,0:T(8,128)S(1)} %fusion.96), custom_call_target="Cholesky" | custom-call | tf_op jit(solution)/shard_map/jit(cholesky)/cholesky | solution.py:38
  388.9 4.9 custom-call.56
  393.8 1.7 fusion.58
  395.5 1.7 fusion.93
  398.5 6.6 %cholesky.333 = f32[64,64]{1,0:T(8,128)S(1)} custom-call(f32[64,64]{1,0:T(8,128)} %fusion.92), custom_call_target="Cholesky" | custom-call | tf_op jit(solution)/shard_map/jit(cholesky)/cholesky | solution.py:44
  406.4 5.5 %custom-call.52 = f32[1,64,64]{1,2,0:T(8,128)} custom-call(f32[1,64,64]{2,1,0:T(8,128)S(1)} %fusion.83), custom_call_target="InvertDiagBlocksLowerTriangular" | custom-call | tf_op jit(solution)/shard_map/jit(_cho_solve)/triangular_solve | solution.py:45
  412.0 6.6 %fusion.119 = f32[512,64]{0,1:T(8,128)S(1)} fusion(f32[2048,512]{0,1:T(8,128)} %get-tuple-element.31, f32[2048,64]{0,1:T(8,128)} %get-tuple-element.32), kind=kOutput, calls=%fused_computation.197 | convolution fusion | flops 805306368 | bytes 4849664 | tf_op jit(solution)/shard_map/dot_general | solution.py:10
  423.0 3.1 convolution_subtract_fusion
  429.1 40.4 %psum.39 = f32[64,64]{0,1:T(8,128)S(1)} all-reduce(f32[64,64]{0,1:T(8,128)S(1)} %fusion.122), channel_id=1, replica_groups=mesh['rows'=8,'grp'=4] {'rows','grp'}, use_global_device_ids=true, to_apply=%region_14.18 | all-reduce | flops 4096 | bytes 32768 | tf_op jit(solution)/shard_map/psum | solution.py:47
  469.6 5.8 %cholesky.344 = f32[64,64]{1,0:T(8,128)S(1)} custom-call(f32[64,64]{1,0:T(8,128)S(1)} %fusion.87), custom_call_target="Cholesky" | custom-call | tf_op jit(solution)/shard_map/jit(cholesky)/cholesky | solution.py:48
  478.6 4.9 custom-call.58
  (140 shorter events, 39.7 us)
Async XLA Ops:
  7.2 1.6 copy-start
  7.2 6.6 %copy-start.6 = (f32[256,512]{1,0:T(8,128)S(1)}, f32[256,512]{1,0:T(8,128)}, u32[]{:S(2)}) copy-start(f32[256,512]{1,0:T(8,128)} %param.11) | copy-start | bytes 1572868
  7.2 166.2 %all-reduce.5.cloned.1.call-start = ((), (), s32[]{:S(2)}) async-start(), calls=%async_computation | async-start | bytes 10485760 | tf_op jit(solution)/shard_map/psum | solution.py:27
  22.1 0.9 copy-start.15
  185.7 1.0 copy-start.9
  269.8 4.2 copy-start.5
  286.3 54.0 %copy-start.3 = (f32[512,512]{1,0:T(8,128)}, f32[512,512]{1,0:T(8,128)S(1)}, u32[]{:S(2)}) copy-start(f32[512,512]{1,0:T(8,128)S(1)} %get-tuple-element.112) | copy-start | bytes 3145732
  326.5 10.1 %copy-start.1 = (f32[2048,512]{0,1:T(8,128)S(1)}, f32[2048,512]{0,1:T(8,128)}, u32[]{:S(2)}) copy-start(f32[2048,512]{0,1:T(8,128)} %get-tuple-element.31) | copy-start | bytes 12582916
  326.5 10.1 %copy-start.11 = (f32[2048,64]{0,1:T(8,128)S(1)}, f32[2048,64]{0,1:T(8,128)}, u32[]{:S(2)}) copy-start(f32[2048,64]{0,1:T(8,128)} %get-tuple-element.33) | copy-start | bytes 1572868
  333.1 7.2 %copy-start.7 = (f32[256,512]{1,0:T(8,128)S(1)}, f32[256,512]{1,0:T(8,128)}, u32[]{:S(2)}) copy-start(f32[256,512]{1,0:T(8,128)} %param.11) | copy-start | bytes 1572868
  333.1 7.2 %copy-start.20 = (f32[256,64]{0,1:T(8,128)S(1)}, f32[256,64]{0,1:T(8,128)}, u32[]{:S(2)}) copy-start(f32[256,64]{0,1:T(8,128)} %copy.20) | copy-start | bytes 196612
  336.1 61.1 %copy-start.13 = (f32[128,64]{0,1:T(8,128)}, f32[128,64]{0,1:T(8,128)S(1)}, u32[]{:S(2)}) copy-start(f32[128,64]{0,1:T(8,128)S(1)} %fusion.73) | copy-start | bytes 98308
  336.7 4.3 copy-start.17
  341.0 0.6 copy-start.12
  397.2 25.7 %copy-start.10 = (f32[2048,64]{0,1:T(8,128)S(1)}, f32[2048,64]{0,1:T(8,128)}, u32[]{:S(2)}) copy-start(f32[2048,64]{0,1:T(8,128)} %get-tuple-element.32) | copy-start | bytes 1572868
  412.0 8.1 %copy-start.4 = (f32[512,512]{1,0:T(8,128)S(1)}, f32[512,512]{1,0:T(8,128)}, u32[]{:S(2)}) copy-start(f32[512,512]{1,0:T(8,128)} %copy-done.3) | copy-start | bytes 3145732
  412.0 11.0 %copy-start.2 = (f32[2048,512]{0,1:T(8,128)S(1)}, f32[2048,512]{0,1:T(8,128)}, u32[]{:S(2)}) copy-start(f32[2048,512]{0,1:T(8,128)} %get-tuple-element.31) | copy-start | bytes 12582916
  420.3 6.3 %copy-start.21 = (f32[1,64,64]{1,2,0:T(8,128)S(1)}, f32[1,64,64]{1,2,0:T(8,128)}, u32[]{:S(2)}) copy-start(f32[1,64,64]{1,2,0:T(8,128)} %custom-call.52) | copy-start | bytes 49156
  420.5 6.6 %copy-start.8 = (f32[256,512]{1,0:T(8,128)S(1)}, f32[256,512]{1,0:T(8,128)}, u32[]{:S(2)}) copy-start(f32[256,512]{1,0:T(8,128)} %param.11) | copy-start | bytes 1572868
  420.5 6.6 %copy-start.19 = (f32[256,64]{0,1:T(8,128)S(1)}, f32[256,64]{0,1:T(8,128)}, u32[]{:S(2)}) copy-start(f32[256,64]{0,1:T(8,128)} %copy.21) | copy-start | bytes 196612
  422.4 4.7 copy-start.14
  423.0 4.1 copy-start.18
  426.1 57.7 %copy-start.16 = (f32[64,256]{1,0:T(8,128)S(1)}, f32[64,256]{1,0:T(8,128)}, u32[]{:S(2)}) copy-start(f32[64,256]{1,0:T(8,128)} %fusion.58) | copy-start | bytes 196612
Sparse Core Ops, SparseCore 0:
  22.2 151.1 all-reduce.4
where the time goes:
time: 500 us; the launch traced here: 492 us
  other arithmetic  162 us (32%)
  waiting for transfers between devices  149 us (30%)
  blocking collectives  79.6 us (16%)
  matrix products  62 us (12%)
  local copies, waits for them, and re-layouts  20.1 us (4%)
  between operations  19.3 us (4%)
    psum x1, waiting for transfers between devices, shards(): prior_sketch = lax.psum(local_prior, ('rows', 'grp'))  149 us
    another operation x14, other arithmetic, shards(): prior_factor = jnp.linalg.cholesky(gram_prior)  79 us
    dot_general x14, matrix products, matmul(): return jnp.dot(left, right, precision=lax.Precision.HIGHEST)  44.9 us
    another operation x4, other arithmetic, shards(): jax.scipy.linalg.cho_solve((prior_factor, True), matmul(prior_sketch.T, s...  41.7 us
    psum x1, blocking collectives, shards(): gram_second = lax.psum(matmul(final_two.T, final_two), ('rows', 'grp'))  40.4 us
    psum x1, blocking collectives, shards(): gram_first = lax.psum(matmul(resid_one.T, resid_one), ('rows', 'grp'))  39.2 us
    another operation x13, local copies, waits for them, and re-layouts, shards(): jax.scipy.linalg.cho_solve((prior_factor, True), matmul(prior_sketch.T, s...  10.7 us
  transfers between devices with their start and end apart: 1, of which 1 were waited for; matrix products, arithmetic and copies ran while one was open for 0% of the time, Pallas kernels for 0%

commit v1 on v0

v1 whole, which is shorter than its diff:
```python
import functools

import jax
import jax.numpy as jnp
from jax import lax
from jax.experimental import pallas as pl
from jax.experimental.pallas import tpu as pltpu
from jax.sharding import PartitionSpec as P

P_SIZE = 64
T = 128
HIGHEST = lax.Precision.HIGHEST
F32 = jnp.float32
VMEM_LIMIT = 60 * 1024 * 1024


def dot(a, b, ca=1, cb=0):
    return lax.dot_general(
        a, b, (((ca,), (cb,)), ((), ())), precision=HIGHEST, preferred_element_type=F32
    )


def bits_of(size):
    out, b = [], 1
    while b < size:
        out.append(b)
        b *= 2
    return out


def orders(rows, grp):
    core = [("grp", b) for b in bits_of(grp)[:1]]
    y = [("grp", b) for b in bits_of(grp)[1:]]
    x = [("rows", b) for b in bits_of(rows)[:1]]
    z = [("rows", b) for b in bits_of(rows)[1:]]
    return core + x + y + z, core + y + x + z, core + z + x + y


def my_bit(axis, b):
    return (lax.axis_index(axis) // b) % 2


def peer(axis, b):
    me = lax.axis_index(axis)
    return {axis: me + b * (1 - 2 * my_bit(axis, b))}


def barrier_all(order):
    sem = pltpu.get_barrier_semaphore()
    for axis, b in order:
        pl.semaphore_signal(sem, inc=1, device_id=peer(axis, b), device_id_type=pl.DeviceIdType.MESH)
    pl.semaphore_wait(sem, len(order))


def remote(src, dst, send, recv, axis, b):
    return pltpu.make_async_remote_copy(
        src_ref=src, dst_ref=dst, send_sem=send, recv_sem=recv,
        device_id=peer(axis, b), device_id_type=pl.DeviceIdType.MESH,
    )


def block_at(order, target, n):
    k = len(order)
    spots = []
    for blk in range(n):
        value = {target[i]: (blk >> (k - 1 - i)) & 1 for i in range(k)}
        spots.append(sum(value[order[i]] << (k - 1 - i) for i in range(k)))
    return spots


def load_columns(idx_ref, cnt_ref, prior_ref, block_ref):
    width = prior_ref.shape[1]
    lane = lax.broadcasted_iota(jnp.int32, prior_ref.shape, 1)
    masked = jnp.where(lane < cnt_ref[0], prior_ref[...], 0.0)
    start = idx_ref[0]
    chosen = block_ref[:, 0:2 * P_SIZE]
    for s in range(1, block_ref.shape[1] // P_SIZE - 1):
        chosen = jnp.where(start == s, block_ref[:, s * P_SIZE:(s + 2) * P_SIZE], chosen)
    return masked, chosen


def reduce_scatter(parts, sems, base):
    k = len(parts[0][0])
    offs = [0] * len(parts)
    size = [acc.shape[0] for _, acc, _ in parts]
    pend = [None] * len(parts)
    send_sem, recv_sem = sems

    def start(q, i):
        order, acc, recvs = parts[q]
        axis, b = order[i]
        half = size[q] // 2
        bit = my_bit(axis, b)
        src = acc.at[pl.ds(pl.multiple_of(offs[q] + (1 - bit) * half, 8), half)]
        c = remote(src, recvs[i], send_sem.at[base + q, i], recv_sem.at[base + q, i], axis, b)
        c.start()
        offs[q] = offs[q] + bit * half
        size[q] = half
        pend[q] = c

    for q in range(len(parts)):
        start(q, 0)
    for i in range(k):
        for q in range(len(parts)):
            pend[q].wait()
            _, acc, recvs = parts[q]
            spot = pl.ds(pl.multiple_of(offs[q], 8), size[q])
            acc[spot] = acc[spot] + recvs[i][...]
            if i + 1 < k:
                start(q, i + 1)
    return offs, size


def gather(parts, offs, size, sems, base):
    k = len(parts[0][0])
    send_sem, recv_sem = sems
    offs, size = list(offs), list(size)
    pend = [None] * len(parts)

    def start(q, i):
        order, full = parts[q]
        axis, b = order[i]
        spot = pl.ds(pl.multiple_of(offs[q], 8), size[q])
        c = remote(full.at[spot], full.at[spot], send_sem.at[base + q, i], recv_sem.at[base + q, i], axis, b)
        c.start()
        offs[q] = offs[q] - my_bit(axis, b) * size[q]
        size[q] = size[q] * 2
        pend[q] = c

    for q in range(len(parts)):
        start(q, k - 1)
    for i in range(k - 1, -1, -1):
        for q in range(len(parts)):
            pend[q].wait()
            if i > 0:
                start(q, i - 1)


def gram_kernel(rows, grp, n_k, cols, grows, *refs):
    idx_ref, cnt_ref, sketch_ref, prior_ref, block_ref, full_a, full_b = refs[:7]
    rest = list(refs[7:])
    n = rows * grp
    ords = orders(rows, grp)
    accs = [rest.pop(0) for _ in cols]
    recvs = [[rest.pop(0) for _ in range(n_k)] for _ in cols]
    gaccs = [rest.pop(0) for _ in range(2)]
    grecvs = [[rest.pop(0) for _ in range(n_k)] for _ in range(2)]
    send_sem, recv_sem = rest
    sems = (send_sem, recv_sem)
    barrier_all(ords[0])
    masked, chosen = load_columns(idx_ref, cnt_ref, prior_ref, block_ref)
    right = jnp.concatenate([masked, chosen], axis=1)
    sk = sketch_ref.shape[0]
    per = sk // n
    step = 512
    for r in range(0, sk, step):
        prod = dot(sketch_ref[r:r + step, :], right)
        lane = 0
        for q, w in enumerate(cols):
            spots = block_at(ords[q], ords[0], n)
            if q == 0:
                accs[q][r:r + step, :] = prod[:, lane:lane + w]
            else:
                for blk in range(r // per, (r + step) // per):
                    s = spots[blk] * per
                    accs[q][s:s + per, :] = prod[blk * per - r:(blk + 1) * per - r, lane:lane + w]
            lane += w
    offs, size = reduce_scatter(
        [(ords[q], accs[q], recvs[q]) for q in range(len(cols))], sems, 0
    )
    mine = jnp.concatenate(
        [accs[q][pl.ds(pl.multiple_of(offs[q], 8), per)] for q in range(len(cols))], axis=1
    )
    gram = dot(mine, mine, 0, 0)
    width = gram.shape[0] // T
    t = 0
    per_part = 8
    for i in range(width):
        for j in range(i + 1):
            q, s = t // per_part, (t % per_part) * T
            gaccs[q][s:s + T, :] = gram[i * T:(i + 1) * T, j * T:(j + 1) * T]
            t += 1
    for q in range(2):
        used = min(per_part, t - q * per_part) * T
        if used < grows:
            gaccs[q][used:grows, :] = jnp.zeros((grows - used, T), F32)
    parts = [(ords[q], gaccs[q], grecvs[q]) for q in range(2)]
    offs, size = reduce_scatter(parts, sems, len(cols))
    for q, full in enumerate((full_a, full_b)):
        spot = pl.ds(pl.multiple_of(offs[q], 8), size[q])
        full[spot] = gaccs[q][spot]
    gather([(ords[0], full_a), (ords[1], full_b)], offs, size, sems, len(cols) + 2)


def solve_kernel(idx_ref, cnt_ref, prior_ref, block_ref, ta_ref, tb_ref,
                 coef_ref, x_ref, resid_ref, gram_ref, a_ref, inv_ref):
    width = prior_ref.shape[1]
    blocks = width // T + 1
    t = 0
    for i in range(blocks):
        for j in range(i + 1):
            src, s = (ta_ref, t * T) if t < 8 else (tb_ref, (t - 8) * T)
            tile = src[s:s + T, :]
            if i == j and i < blocks - 1:
                row = lax.broadcasted_iota(jnp.int32, (T, T), 0)
                col = lax.broadcasted_iota(jnp.int32, (T, T), 1)
                tile = tile + jnp.where((row == col) & (row + i * T >= cnt_ref[0]), 1.0, 0.0)
            a_ref[i * T:(i + 1) * T, j * T:(j + 1) * T] = tile
            if i != j:
                a_ref[j * T:(j + 1) * T, i * T:(i + 1) * T] = tile.T
            t += 1

    lane = lax.broadcasted_iota(jnp.int32, (T, T), 1)
    sub = lax.broadcasted_iota(jnp.int32, (8, T), 0)
    lane8 = lax.broadcasted_iota(jnp.int32, (1, T), 1)

    def body(k, _):
        at = pl.ds(pl.multiple_of(k * T, T), T)
        d = a_ref[at, at]
        tiles = [d[8 * v:8 * v + 8, :] for v in range(T // 8)]
        for p in range(T):
            v, o = p // 8, p % 8
            row = tiles[v][o:o + 1, :]
            piv = 1.0 / row[:, p:p + 1]
            row = jnp.where(lane8 == p, piv, row * piv)
            new = []
            for u in range(T // 8):
                col = tiles[u][:, p:p + 1]
                base = jnp.where(lane8 == p, 0.0, tiles[u])
                w = base - col * row
                if u == v:
                    w = jnp.where(sub == o, row, w)
                new.append(w)
            tiles = new
        inv = jnp.concatenate(tiles, axis=0)
        rowk = dot(inv, a_ref[at, :])
        colk = a_ref[:, at]
        a_ref[...] = a_ref[...] - dot(colk, rowk)
        a_ref[at, :] = rowk
        return 0

    lax.fori_loop(0, blocks - 1, body, 0)
    coef = a_ref[0:width, width:width + T]
    coef_ref[...] = coef
    e = a_ref[width:width + P_SIZE, width:width + T]
    tiles = [e[8 * v:8 * v + 8, :] for v in range(P_SIZE // 8)]
    for p in range(P_SIZE):
        v, o = p // 8, p % 8
        row = tiles[v][o:o + 1, :]
        row = row / row[:, p:p + 1]
        new = []
        for u in range(P_SIZE // 8):
            w = tiles[u] - tiles[u][:, p:p + 1] * row
            if u == v:
                w = jnp.where(sub == o, row, w)
            new.append(w)
        tiles = new
    x = jnp.concatenate(tiles, axis=0)[:, P_SIZE:]
    x_ref[...] = x
    masked, chosen = load_columns(idx_ref, cnt_ref, prior_ref, block_ref)
    resid = chosen - dot(masked, coef)
    one = resid[:, :P_SIZE]
    two = resid[:, P_SIZE:] - dot(one, x)
    resid_ref[...] = jnp.concatenate([one, two], axis=1)
    gram_ref[...] = jnp.concatenate([dot(one, one, 0, 0), dot(two, two, 0, 0)], axis=1)


def finish_kernel(order, scale, gram_ref, resid_ref, x_ref, coef_ref, basis_ref, factors_ref,
                  hold, recv, send_sem, recv_sem):
    barrier_all(order)
    k = len(order)
    for i, (axis, b) in enumerate(order):
        src = gram_ref if i == 0 else hold.at[i - 1]
        c = remote(src, recv.at[i], send_sem.at[i], recv_sem.at[i], axis, b)
        c.start()
        c.wait()
        hold[i] = src[...] + recv[i]
    gram = hold[k - 1]
    eye = (lax.broadcasted_iota(jnp.int32, (P_SIZE, P_SIZE), 0)
           == lax.broadcasted_iota(jnp.int32, (P_SIZE, P_SIZE), 1)).astype(F32)
    sub = lax.broadcasted_iota(jnp.int32, (8, T), 0)
    mats = []
    for h in range(2):
        m = jnp.concatenate([gram[:, h * P_SIZE:(h + 1) * P_SIZE], eye], axis=1)
        mats.append([m[8 * v:8 * v + 8, :] for v in range(P_SIZE // 8)])
    for p in range(P_SIZE):
        v, o = p // 8, p % 8
        for h in range(2):
            tiles = mats[h]
            row = tiles[v][o:o + 1, :]
            d = row[:, p:p + 1]
            y = lax.rsqrt(d)
            y = y * (1.5 - 0.5 * d * y * y)
            row = row * y
            new = list(tiles)
            for u in range(v, P_SIZE // 8):
                w = tiles[u] - (tiles[u][:, p:p + 1] * y) * row
                if u == v:
                    w = jnp.where(sub == o, row, jnp.where(sub > o, w, tiles[u]))
                new[u] = w
            mats[h] = new
    full = [jnp.concatenate(m, axis=0) for m in mats]
    row = lax.broadcasted_iota(jnp.int32, (P_SIZE, P_SIZE), 0)
    col = lax.broadcasted_iota(jnp.int32, (P_SIZE, P_SIZE), 1)
    upper = [jnp.where(row <= col, f[:, :P_SIZE], 0.0) for f in full]
    lowinv = [f[:, P_SIZE:] for f in full]
    basis_ref[...] = jnp.concatenate(
        [dot(resid_ref[:, h * P_SIZE:(h + 1) * P_SIZE], lowinv[h], 1, 1) for h in range(2)], axis=1
    ) * scale
    width = coef_ref.shape[0]
    factors_ref[0:width, :] = coef_ref[...]
    inner = dot(upper[0], x_ref[...])
    factors_ref[width:width + P_SIZE, :] = jnp.concatenate([upper[0], inner], axis=1)
    factors_ref[width + P_SIZE:, :] = jnp.concatenate([jnp.zeros_like(eye), upper[1]], axis=1)


def shards(rows, grp, sketch, prior, block, idx, cnt):
    n = rows * grp
    n_k = len(orders(rows, grp)[0])
    sk, local = sketch.shape
    width = prior.shape[1]
    vm = pl.BlockSpec(memory_space=pltpu.VMEM)
    sm = pl.BlockSpec(memory_space=pltpu.SMEM)
    cols = (2 * T, 2 * T, width + T - 4 * T)
    grows = n * max(8, 8 * T // n)
    scratch = [pltpu.VMEM((sk, w), F32) for w in cols]
    for w in cols:
        scratch += [pltpu.VMEM((sk >> (i + 1), w), F32) for i in range(n_k)]
    scratch += [pltpu.VMEM((grows, T), F32)] * 2
    for _ in range(2):
        scratch += [pltpu.VMEM((grows >> (i + 1), T), F32) for i in range(n_k)]
    scratch += [pltpu.SemaphoreType.DMA((7, n_k))] * 2
    tiles = pl.pallas_call(
        functools.partial(gram_kernel, rows, grp, n_k, cols, grows),
        out_shape=[jax.ShapeDtypeStruct((grows, T), F32)] * 2,
        in_specs=[sm, sm, vm, vm, vm],
        out_specs=[vm, vm],
        scratch_shapes=scratch,
        compiler_params=pltpu.CompilerParams(
            collective_id=0, has_side_effects=True, vmem_limit_bytes=VMEM_LIMIT
        ),
    )(idx, cnt, sketch, prior, block)
    coef, x, resid, gram = pl.pallas_call(
        solve_kernel,
        out_shape=[
            jax.ShapeDtypeStruct((width, T), F32),
            jax.ShapeDtypeStruct((P_SIZE, P_SIZE), F32),
            jax.ShapeDtypeStruct((local, T), F32),
            jax.ShapeDtypeStruct((P_SIZE, T), F32),
        ],
        in_specs=[sm, sm, vm, vm, vm, vm],
        out_specs=[vm] * 4,
        scratch_shapes=[pltpu.VMEM((width + T, width + T), F32), pltpu.VMEM((T, T), F32)],
        compiler_params=pltpu.CompilerParams(vmem_limit_bytes=VMEM_LIMIT),
    )(idx, cnt, prior, block, *tiles)
    order = orders(rows, grp)[0]
    scale = float(local * n) ** 0.5
    return tuple(pl.pallas_call(
        functools.partial(finish_kernel, order, scale),
        out_shape=[
            jax.ShapeDtypeStruct((local, T), F32),
            jax.ShapeDtypeStruct((width + T, T), F32),
        ],
        in_specs=[vm] * 4,
        out_specs=[vm] * 2,
        scratch_shapes=[
            pltpu.VMEM((n_k, P_SIZE, T), F32),
            pltpu.VMEM((n_k, P_SIZE, T), F32),
            pltpu.SemaphoreType.DMA((n_k,)),
            pltpu.SemaphoreType.DMA((n_k,)),
        ],
        compiler_params=pltpu.CompilerParams(
            collective_id=1, has_side_effects=True, vmem_limit_bytes=VMEM_LIMIT
        ),
    )(gram, resid, x, coef))


def solution(mesh):
    rows, grp = mesh.shape["rows"], mesh.shape["grp"]
    placed = (
        P(None, ("rows", "grp")),
        P(("rows", "grp"), None),
        P(("rows", "grp"), None),
        P(),
        P(),
    )
    return jax.shard_map(
        functools.partial(shards, rows, grp),
        mesh=mesh,
        in_specs=placed,
        out_specs=(P(("rows", "grp"), None), P()),
        check_vma=False,
    )
```

time: 500 us -> 171 us (0.34); the launches traced: 492 us -> 171 us
  Pallas kernels: 0 us -> 166 us
  other arithmetic: 162 us -> 0 us
  waiting for transfers between devices: 149 us -> 0 us
  blocking collectives: 79.6 us -> 0 us
  matrix products: 62 us -> 0 us
  between operations: 19.3 us -> 1.94 us
  local copies, waits for them, and re-layouts: 20.1 us -> 3.29 us
    pallas_call x0 -> x3, Pallas kernels: none -> 166 us  [the longest x1 81.5 us: shards(): pl.pallas_call(functools.partial(gram_kernel, rows, grp, n_k, cols, grows...]
    another operation x31 -> x0, other arithmetic: 157 us -> none  [the longest x14 79 us: shards(): prior_factor = jnp.linalg.cholesky(gram_prior)]
    psum x1 -> x0, waiting for transfers between devices: 149 us -> none  [shards(): prior_sketch = lax.psum(local_prior, ('rows', 'grp'))]
    psum x2 -> x0, blocking collectives: 79.6 us -> none  [the longest x1 40.4 us: shards(): gram_second = lax.psum(matmul(final_two.T, final_two), ('rows', 'grp'))]
    dot_general x14 -> x0, matrix products: 44.9 us -> none  [matmul(): return jnp.dot(left, right, precision=lax.Precision.HIGHEST)]
    another operation x39 -> x0, matrix products: 17.2 us -> none  [the longest x28 7.65 us: shards(): jax.scipy.linalg.cho_solve((prior_factor, True), matmul(prior_sketch.T, s...]
    another operation x18 -> x0, local copies, waits for them, and re-layouts: 11 us -> none  [the longest x13 10.7 us: shards(): jax.scipy.linalg.cho_solve((prior_factor, True), matmul(prior_sketch.T, s...]
  transfers between devices with their start and end apart: 1 -> 0, of which waited for: 1 -> 0; matrix products, arithmetic and copies ran while one was open for 0% -> 0% of each run, Pallas kernels for 0% -> 0%
where the time goes in v1:
time: 171 us
  Pallas kernels  166 us (97%)
  local copies, waits for them, and re-layouts  3.29 us (2%)
  between operations  1.94 us (1%)
    pallas_call x1, Pallas kernels, shards(): pl.pallas_call(functools.partial(gram_kernel, rows, grp, n_k, cols, grows...  81.5 us
    pallas_call x1, Pallas kernels, shards(): pl.pallas_call(solve_kernel, out_shape=[jax.ShapeDtypeStruct((width, T),...  60.2 us
    pallas_call x1, Pallas kernels, shards(): pl.pallas_call(functools.partial(finish_kernel, order, scale), out_shape=...  24 us

profile of v1, /device:TPU:0, one launch (start us, length us, event | category | flops | bytes accessed | tf_op | source)
XLA Modules:
  0.0 171.1 jit_solution(14913750158797859356)
XLA Ops:
  1.9 81.5 %shard_map.68 = (f32[1024,128]{1,0:T(8,128)}, f32[1024,128]{1,0:T(8,128)}) custom-call(s32[1]{0:T(128)S(6)} %copy.9.refs_0_.idx_ref, s32[1]{0:T(128)S(6)} %copy.10.refs_1_.cnt_ref, f32[2048,256]{1,0:T(8,128)} %refs_2_.1, f32[256,512]{1,0:T(8,128)} %prior_ref.1, f32[256,256]{1,0:T(8,128)} %block_ref.1), custom_call_target="tpu_custom_call" | custom-call | tf_op jit(solution)/shard_map/pallas_call | solution.py:333
  83.5 60.2 %shard_map.69 = (f32[512,128]{1,0:T(8,128)}, f32[64,64]{1,0:T(8,128)}, f32[256,128]{1,0:T(8,128)}, f32[64,128]{1,0:T(8,128)}) custom-call(s32[1]{0:T(128)S(6)} %copy.9.refs_0_.idx_ref, s32[1]{0:T(128)S(6)} %copy.10.refs_1_.cnt_ref, f32[256,512]{1,0:T(8,128)} %prior_ref.1, f32[256,256]{1,0:T(8,128)} %block_ref.1, f32[1024,128]{1,0:T(8,128)} %get-tuple-element.8.ta_ref, ...), custom_call_target="tpu_custom_call" | custom-call | tf_op jit(solution)/shard_map/pallas_call | solution.py:343
  143.7 24.0 %shard_map.70 = (f32[256,128]{1,0:T(8,128)}, f32[640,128]{1,0:T(8,128)}) custom-call(f32[64,128]{1,0:T(8,128)} %get-tuple-element.10.gram_ref, f32[256,128]{1,0:T(8,128)} %get-tuple-element.11.resid_ref, f32[64,64]{1,0:T(8,128)} %get-tuple-element.12.x_ref, f32[512,128]{1,0:T(8,128)} %get-tuple-element.13.coef_ref), custom_call_target="tpu_custom_call" | custom-call | tf_op jit(solution)/shard_map/pallas_call | solution.py:358
  167.8 1.6 copy.11
  169.3 1.7 %copy.12 = f32[640,128]{1,0:T(8,128)} copy(f32[640,128]{1,0:T(8,128)} %get-tuple-element.17) | data formatting | bytes 655360

commit v2 on v1

--- a/solution.py
+++ b/solution.py
@@ -18,6 +18,19 @@
     return lax.dot_general(
         a, b, (((ca,), (cb,)), ((), ())), precision=HIGHEST, preferred_element_type=F32
     )
+
+
+def split(x):
+    hi = x.astype(jnp.bfloat16)
+    return hi, (x - hi.astype(F32)).astype(jnp.bfloat16)
+
+
+def dot3(a, b):
+    ah, al = a
+    bh, bl = b
+    out = jnp.dot(ah, bl, preferred_element_type=F32)
+    out = out + jnp.dot(al, bh, preferred_element_type=F32)
+    return out + jnp.dot(ah, bh, preferred_element_type=F32)
 
 
 def bits_of(size):
@@ -149,12 +162,12 @@
     sems = (send_sem, recv_sem)
     barrier_all(ords[0])
     masked, chosen = load_columns(idx_ref, cnt_ref, prior_ref, block_ref)
-    right = jnp.concatenate([masked, chosen], axis=1)
+    right = split(jnp.concatenate([masked, chosen], axis=1))
     sk = sketch_ref.shape[0]
     per = sk // n
     step = 512
     for r in range(0, sk, step):
-        prod = dot(sketch_ref[r:r + step, :], right)
+        prod = dot3(split(sketch_ref[r:r + step, :]), right)
         lane = 0
         for q, w in enumerate(cols):
             spots = block_at(ords[q], ords[0], n)
@@ -192,6 +205,45 @@
     gather([(ords[0], full_a), (ords[1], full_b)], offs, size, sems, len(cols) + 2)
 
 
+def sweep4(tiles, p, inverse):
+    v, o = p // 8, p % 8
+    lane = lax.broadcasted_iota(jnp.int32, (8, T), 1)
+    sub = lax.broadcasted_iota(jnp.int32, (8, T), 0)
+    r = [jnp.broadcast_to(tiles[v][o + i:o + i + 1, :], (8, T)) for i in range(4)]
+
+    def at(i, j):
+        return jnp.broadcast_to(r[i][:, p + j:p + j + 1], (8, T))
+
+    a, b, e, f = at(0, 0), at(0, 1), at(0, 2), at(0, 3)
+    c, g, h = at(1, 1), at(1, 2), at(1, 3)
+    x, y, z = at(2, 2), at(2, 3), at(3, 3)
+    ra = 1.0 / (a * c - b * b)
+    k00, k01 = (c * e - b * g) * ra, (c * f - b * h) * ra
+    k10, k11 = (a * g - b * e) * ra, (a * h - b * f) * ra
+    s00 = x - (e * k00 + g * k10)
+    s01 = y - (e * k01 + g * k11)
+    s11 = z - (f * k01 + h * k11)
+    rs = 1.0 / (s00 * s11 - s01 * s01)
+    inside = (lane >= p) & (lane < p + 4)
+    if inverse:
+        r = [jnp.where(inside, jnp.where(lane == p + i, 1.0, 0.0), r[i]) for i in range(4)]
+    g0, g1 = (c * r[0] - b * r[1]) * ra, (a * r[1] - b * r[0]) * ra
+    q2 = r[2] - (k00 * r[0] + k10 * r[1])
+    q3 = r[3] - (k01 * r[0] + k11 * r[1])
+    n2, n3 = (s11 * q2 - s01 * q3) * rs, (s00 * q3 - s01 * q2) * rs
+    n0, n1 = g0 - (k00 * n2 + k01 * n3), g1 - (k10 * n2 + k11 * n3)
+    new = []
+    for u, tile in enumerate(tiles):
+        w = jnp.where(inside, 0.0, tile) if inverse else tile
+        for j, row in enumerate((n0, n1, n2, n3)):
+            w = w - tile[:, p + j:p + j + 1] * row
+        if u == v:
+            for j, row in enumerate((n0, n1, n2, n3)):
+                w = jnp.where(sub == o + j, row, w)
+        new.append(w)
+    return new
+
+
 def solve_kernel(idx_ref, cnt_ref, prior_ref, block_ref, ta_ref, tb_ref,
                  coef_ref, x_ref, resid_ref, gram_ref, a_ref, inv_ref):
     width = prior_ref.shape[1]
@@ -210,33 +262,23 @@
                 a_ref[j * T:(j + 1) * T, i * T:(i + 1) * T] = tile.T
             t += 1
 
-    lane = lax.broadcasted_iota(jnp.int32, (T, T), 1)
-    sub = lax.broadcasted_iota(jnp.int32, (8, T), 0)
-    lane8 = lax.broadcasted_iota(jnp.int32, (1, T), 1)
-
     def body(k, _):
         at = pl.ds(pl.multiple_of(k * T, T), T)
         d = a_ref[at, at]
         tiles = [d[8 * v:8 * v + 8, :] for v in range(T // 8)]
-        for p in range(T):
-            v, o = p // 8, p % 8
-            row = tiles[v][o:o + 1, :]
-            piv = 1.0 / row[:, p:p + 1]
-            row = jnp.where(lane8 == p, piv, row * piv)
-            new = []
-            for u in range(T // 8):
-                col = tiles[u][:, p:p + 1]
-                base = jnp.where(lane8 == p, 0.0, tiles[u])
-                w = base - col * row
-                if u == v:
-                    w = jnp.where(sub == o, row, w)
-                new.append(w)
-            tiles = new
-        inv = jnp.concatenate(tiles, axis=0)
-        rowk = dot(inv, a_ref[at, :])
-        colk = a_ref[:, at]
-        a_ref[...] = a_ref[...] - dot(colk, rowk)
-        a_ref[at, :] = rowk
+        for p in range(0, T, 4):
+            tiles = sweep4(tiles, p, True)
+        inv_ref[...] = jnp.concatenate(tiles, axis=0)
+        for kk in range(blocks - 1):
+            @pl.when(k == kk)
+            def _():
+                own, rest = slice(kk * T, (kk + 1) * T), slice((kk + 1) * T, blocks * T)
+                rowk = dot(inv_ref[...], a_ref[own, rest])
+                if kk:
+                    top = slice(0, kk * T)
+                    a_ref[top, rest] = a_ref[top, rest] - dot(a_ref[top, own], rowk)
+                a_ref[rest, rest] = a_ref[rest, rest] - dot(a_ref[rest, own], rowk)
+                a_ref[own, rest] = rowk
         return 0
 
     lax.fori_loop(0, blocks - 1, body, 0)
@@ -244,17 +286,8 @@
     coef_ref[...] = coef
     e = a_ref[width:width + P_SIZE, width:width + T]
     tiles = [e[8 * v:8 * v + 8, :] for v in range(P_SIZE // 8)]
-    for p in range(P_SIZE):
-        v, o = p // 8, p % 8
-        row = tiles[v][o:o + 1, :]
-        row = row / row[:, p:p + 1]
-        new = []
-        for u in range(P_SIZE // 8):
-            w = tiles[u] - tiles[u][:, p:p + 1] * row
-            if u == v:
-                w = jnp.where(sub == o, row, w)
-            new.append(w)
-        tiles = new
+    for p in range(0, P_SIZE, 4):
+        tiles = sweep4(tiles, p, False)
     x = jnp.concatenate(tiles, axis=0)[:, P_SIZE:]
     x_ref[...] = x
     masked, chosen = load_columns(idx_ref, cnt_ref, prior_ref, block_ref)
@@ -265,8 +298,7 @@
     gram_ref[...] = jnp.concatenate([dot(one, one, 0, 0), dot(two, two, 0, 0)], axis=1)
 
 
-def finish_kernel(order, scale, gram_ref, resid_ref, x_ref, coef_ref, basis_ref, factors_ref,
-                  hold, recv, send_sem, recv_sem):
+def sum_kernel(order, gram_ref, out_ref, hold, recv, send_sem, recv_sem):
     barrier_all(order)
     k = len(order)
     for i, (axis, b) in enumerate(order):
@@ -274,8 +306,12 @@
         c = remote(src, recv.at[i], send_sem.at[i], recv_sem.at[i], axis, b)
         c.start()
         c.wait()
-        hold[i] = src[...] + recv[i]
-    gram = hold[k - 1]
+        dst = out_ref if i == k - 1 else hold.at[i]
+        dst[...] = src[...] + recv[i]
+
+
+def finish_kernel(scale, gram_ref, resid_ref, x_ref, coef_ref, basis_ref, factors_ref):
+    gram = gram_ref[...]
     eye = (lax.broadcasted_iota(jnp.int32, (P_SIZE, P_SIZE), 0)
            == lax.broadcasted_iota(jnp.int32, (P_SIZE, P_SIZE), 1)).astype(F32)
     sub = lax.broadcasted_iota(jnp.int32, (8, T), 0)
@@ -355,23 +391,28 @@
     )(idx, cnt, prior, block, *tiles)
     order = orders(rows, grp)[0]
     scale = float(local * n) ** 0.5
+    gram = pl.pallas_call(
+        functools.partial(sum_kernel, order),
+        out_shape=jax.ShapeDtypeStruct((P_SIZE, T), F32),
+        in_specs=[vm],
+        out_specs=vm,
+        scratch_shapes=[
+            pltpu.VMEM((n_k, P_SIZE, T), F32),
+            pltpu.VMEM((n_k, P_SIZE, T), F32),
+            pltpu.SemaphoreType.DMA((n_k,)),
+            pltpu.SemaphoreType.DMA((n_k,)),
+        ],
+        compiler_params=pltpu.CompilerParams(collective_id=1, has_side_effects=True),
+    )(gram)
     return tuple(pl.pallas_call(
-        functools.partial(finish_kernel, order, scale),
+        functools.partial(finish_kernel, scale),
         out_shape=[
             jax.ShapeDtypeStruct((local, T), F32),
             jax.ShapeDtypeStruct((width + T, T), F32),
         ],
         in_specs=[vm] * 4,
         out_specs=[vm] * 2,
-        scratch_shapes=[
-            pltpu.VMEM((n_k, P_SIZE, T), F32),
-            pltpu.VMEM((n_k, P_SIZE, T), F32),
-            pltpu.SemaphoreType.DMA((n_k,)),
-            pltpu.SemaphoreType.DMA((n_k,)),
-        ],
-        compiler_params=pltpu.CompilerParams(
-            collective_id=1, has_side_effects=True, vmem_limit_bytes=VMEM_LIMIT
-        ),
+        compiler_params=pltpu.CompilerParams(vmem_limit_bytes=VMEM_LIMIT),
     )(gram, resid, x, coef))
 
 

time: 171 us -> 148 us (0.87)
  Pallas kernels: 166 us -> 146 us
  local copies, waits for them, and re-layouts: 3.29 us -> 0 us
    pallas_call x1, Pallas kernels: 60.2 us -> 40.6 us  [shards(): pl.pallas_call(solve_kernel, out_shape=[jax.ShapeDtypeStruct((width, T),...]
    unnamed x2 -> x0, local copies, waits for them, and re-layouts: 3.29 us -> none
    pallas_call x1, Pallas kernels: 81.5 us -> 79.6 us  [shards(): pl.pallas_call(functools.partial(gram_kernel, rows, grp, n_k, cols, grows...]
    pallas_call x1 -> x2, Pallas kernels: 24 us -> 25.4 us  [the longest x1 17.2 us: shards(): pl.pallas_call(functools.partial(sum_kernel, order), out_shape=jax.ShapeD...]
where the time goes in v2:
time: 148 us
  Pallas kernels  146 us (99%)
  between operations  1.94 us (1%)
    pallas_call x1, Pallas kernels, shards(): pl.pallas_call(functools.partial(gram_kernel, rows, grp, n_k, cols, grows...  79.6 us
    pallas_call x1, Pallas kernels, shards(): pl.pallas_call(solve_kernel, out_shape=[jax.ShapeDtypeStruct((width, T),...  40.6 us
    pallas_call x1, Pallas kernels, shards(): pl.pallas_call(functools.partial(sum_kernel, order), out_shape=jax.ShapeD...  17.2 us
    pallas_call x1, Pallas kernels, shards(): pl.pallas_call(functools.partial(finish_kernel, scale), out_shape=[jax.Sh...  8.24 us

profile of v2, /device:TPU:0, one launch (start us, length us, event | category | flops | bytes accessed | tf_op | source)
XLA Modules:
  0.0 147.6 jit_solution(16963198755223785168)
XLA Ops:
  1.9 79.6 %shard_map.68 = (f32[1024,128]{1,0:T(8,128)}, f32[1024,128]{1,0:T(8,128)}) custom-call(s32[1]{0:T(128)S(6)} %copy.7.refs_0_.idx_ref, s32[1]{0:T(128)S(6)} %copy.8.refs_1_.cnt_ref, f32[2048,256]{1,0:T(8,128)} %refs_2_.1, f32[256,512]{1,0:T(8,128)} %prior_ref.1, f32[256,256]{1,0:T(8,128)} %block_ref.1), custom_call_target="tpu_custom_call" | custom-call | tf_op jit(solution)/shard_map/pallas_call | solution.py:369
  81.5 40.6 %shard_map.69 = (f32[512,128]{1,0:T(8,128)}, f32[64,64]{1,0:T(8,128)}, f32[256,128]{1,0:T(8,128)}, f32[64,128]{1,0:T(8,128)}) custom-call(s32[1]{0:T(128)S(6)} %copy.7.refs_0_.idx_ref, s32[1]{0:T(128)S(6)} %copy.8.refs_1_.cnt_ref, f32[256,512]{1,0:T(8,128)} %prior_ref.1, f32[256,256]{1,0:T(8,128)} %block_ref.1, f32[1024,128]{1,0:T(8,128)} %get-tuple-element.8.ta_ref, ...), custom_call_target="tpu_custom_call" | custom-call | tf_op jit(solution)/shard_map/pallas_call | solution.py:379
  122.1 17.2 %shard_map.70.gram_ref = f32[64,128]{1,0:T(8,128)} custom-call(f32[64,128]{1,0:T(8,128)} %get-tuple-element.10.gram_ref), custom_call_target="tpu_custom_call" | custom-call | tf_op jit(solution)/shard_map/pallas_call | solution.py:394
  139.3 8.2 %shard_map.71 = (f32[256,128]{1,0:T(8,128)}, f32[640,128]{1,0:T(8,128)}) custom-call(f32[64,128]{1,0:T(8,128)} %shard_map.70.gram_ref, f32[256,128]{1,0:T(8,128)} %get-tuple-element.11.resid_ref, f32[64,64]{1,0:T(8,128)} %get-tuple-element.12.x_ref, f32[512,128]{1,0:T(8,128)} %get-tuple-element.13.coef_ref), custom_call_target="tpu_custom_call" | custom-call | tf_op jit(solution)/shard_map/pallas_call | solution.py:407

commit v3 on v2

--- a/solution.py
+++ b/solution.py
@@ -41,35 +41,124 @@
     return out
 
 
-def orders(rows, grp):
+def axes_of(rows, grp):
     core = [("grp", b) for b in bits_of(grp)[:1]]
     y = [("grp", b) for b in bits_of(grp)[1:]]
     x = [("rows", b) for b in bits_of(rows)[:1]]
     z = [("rows", b) for b in bits_of(rows)[1:]]
-    return core + x + y + z, core + y + x + z, core + z + x + y
+    return core, y, x, z
 
 
 def my_bit(axis, b):
     return (lax.axis_index(axis) // b) % 2
 
 
-def peer(axis, b):
-    me = lax.axis_index(axis)
-    return {axis: me + b * (1 - 2 * my_bit(axis, b))}
-
-
-def barrier_all(order):
+def peer(group, pattern):
+    out = {}
+    for i, (axis, b) in enumerate(group):
+        if (pattern >> (len(group) - 1 - i)) & 1:
+            here = out.get(axis, lax.axis_index(axis))
+            out[axis] = here + b * (1 - 2 * my_bit(axis, b))
+    return out
+
+
+def spot_in(group, pattern=0):
+    k, at = len(group), 0
+    for i, (axis, b) in enumerate(group):
+        flip, bit = (pattern >> (k - 1 - i)) & 1, my_bit(axis, b)
+        at = at + (1 - bit if flip else bit) * (1 << (k - 1 - i))
+    return at
+
+
+def barrier_all(groups):
     sem = pltpu.get_barrier_semaphore()
-    for axis, b in order:
-        pl.semaphore_signal(sem, inc=1, device_id=peer(axis, b), device_id_type=pl.DeviceIdType.MESH)
-    pl.semaphore_wait(sem, len(order))
-
-
-def remote(src, dst, send, recv, axis, b):
+    count = 0
+    for group in groups:
+        for pattern in range(1, 1 << len(group)):
+            pl.semaphore_signal(
+                sem, inc=1, device_id=peer(group, pattern), device_id_type=pl.DeviceIdType.MESH
+            )
+            count += 1
+    pl.semaphore_wait(sem, count)
+
+
+def remote(src, dst, send, recv, group, pattern):
     return pltpu.make_async_remote_copy(
         src_ref=src, dst_ref=dst, send_sem=send, recv_sem=recv,
-        device_id=peer(axis, b), device_id_type=pl.DeviceIdType.MESH,
+        device_id=peer(group, pattern), device_id_type=pl.DeviceIdType.MESH,
     )
+
+
+def rows_at(start, size):
+    return pl.ds(pl.multiple_of(start, 8), size)
+
+
+class Halving:
+    def __init__(self, stages, acc, recvs, sends, arrives, full=None, gsends=None, garrives=None):
+        self.stages, self.acc, self.recvs, self.full = stages, acc, recvs, full
+        self.sems, self.gsems = (sends, arrives), (gsends, garrives)
+        self.off, self.size, self.pend = 0, acc.shape[0], []
+
+    def start(self, i):
+        group = self.stages[i]
+        sub = self.size >> len(group)
+        self.pend = []
+        for m in range(1, 1 << len(group)):
+            src = self.acc.at[rows_at(self.off + spot_in(group, m) * sub, sub)]
+            c = remote(src, self.recvs[i].at[m - 1], self.sems[0].at[i, m - 1],
+                       self.sems[1].at[i, m - 1], group, m)
+            c.start()
+            self.pend.append(c)
+        self.off = self.off + spot_in(group) * sub
+        self.size = sub
+
+    def finish(self, i):
+        for c in self.pend:
+            c.wait()
+        at = rows_at(self.off, self.size)
+        total = self.acc[at]
+        for m in range(len(self.pend)):
+            total = total + self.recvs[i][m]
+        self.acc[at] = total
+
+    def gstart(self, i):
+        group = self.stages[i]
+        self.pend = []
+        at = self.full.at[rows_at(self.off, self.size)]
+        for m in range(1, 1 << len(group)):
+            c = remote(at, at, self.gsems[0].at[i, m - 1], self.gsems[1].at[i, m - 1], group, m)
+            c.start()
+            self.pend.append(c)
+        self.off = self.off - spot_in(group) * self.size
+        self.size = self.size << len(group)
+
+    def gfinish(self):
+        for c in self.pend:
+            c.wait()
+
+
+def recv_shapes(stages, rows, lanes):
+    out = []
+    for group in stages:
+        rows = rows >> len(group)
+        out.append(pltpu.VMEM(((1 << len(group)) - 1, rows, lanes), F32))
+    return out
+
+
+def sem_shape(stages):
+    return pltpu.SemaphoreType.DMA((len(stages), max((1 << len(g)) - 1 for g in stages)))
+
+
+def sketch_plan(rows, grp):
+    core, y, x, z = axes_of(rows, grp)
+    one = lambda bits: [[b] for b in bits]
+    first, second, third = one(core + x + y + z), one(core + y + x + z), one(core + z + x + y)
+    return [first, second, third, first, second]
+
+
+def gram_plan(rows, grp):
+    core, y, x, z = axes_of(rows, grp)
+    return [[g for g in (core, x + y, z) if g], [g for g in (core, z, x + y) if g]]
 
 
 def block_at(order, target, n):
@@ -92,117 +181,83 @@
     return masked, chosen
 
 
-def reduce_scatter(parts, sems, base):
-    k = len(parts[0][0])
-    offs = [0] * len(parts)
-    size = [acc.shape[0] for _, acc, _ in parts]
-    pend = [None] * len(parts)
-    send_sem, recv_sem = sems
-
-    def start(q, i):
-        order, acc, recvs = parts[q]
-        axis, b = order[i]
-        half = size[q] // 2
-        bit = my_bit(axis, b)
-        src = acc.at[pl.ds(pl.multiple_of(offs[q] + (1 - bit) * half, 8), half)]
-        c = remote(src, recvs[i], send_sem.at[base + q, i], recv_sem.at[base + q, i], axis, b)
-        c.start()
-        offs[q] = offs[q] + bit * half
-        size[q] = half
-        pend[q] = c
-
-    for q in range(len(parts)):
-        start(q, 0)
-    for i in range(k):
-        for q in range(len(parts)):
-            pend[q].wait()
-            _, acc, recvs = parts[q]
-            spot = pl.ds(pl.multiple_of(offs[q], 8), size[q])
-            acc[spot] = acc[spot] + recvs[i][...]
-            if i + 1 < k:
-                start(q, i + 1)
-    return offs, size
-
-
-def gather(parts, offs, size, sems, base):
-    k = len(parts[0][0])
-    send_sem, recv_sem = sems
-    offs, size = list(offs), list(size)
-    pend = [None] * len(parts)
-
-    def start(q, i):
-        order, full = parts[q]
-        axis, b = order[i]
-        spot = pl.ds(pl.multiple_of(offs[q], 8), size[q])
-        c = remote(full.at[spot], full.at[spot], send_sem.at[base + q, i], recv_sem.at[base + q, i], axis, b)
-        c.start()
-        offs[q] = offs[q] - my_bit(axis, b) * size[q]
-        size[q] = size[q] * 2
-        pend[q] = c
-
-    for q in range(len(parts)):
-        start(q, k - 1)
-    for i in range(k - 1, -1, -1):
-        for q in range(len(parts)):
-            pend[q].wait()
-            if i > 0:
-                start(q, i - 1)
-
-
-def gram_kernel(rows, grp, n_k, cols, grows, *refs):
-    idx_ref, cnt_ref, sketch_ref, prior_ref, block_ref, full_a, full_b = refs[:7]
-    rest = list(refs[7:])
+def gram_kernel(rows, grp, grows, idx_ref, cnt_ref, sketch_ref, prior_ref, block_ref,
+                full_a, full_b, *rest):
+    rest = list(rest)
     n = rows * grp
-    ords = orders(rows, grp)
-    accs = [rest.pop(0) for _ in cols]
-    recvs = [[rest.pop(0) for _ in range(n_k)] for _ in cols]
-    gaccs = [rest.pop(0) for _ in range(2)]
-    grecvs = [[rest.pop(0) for _ in range(n_k)] for _ in range(2)]
-    send_sem, recv_sem = rest
-    sems = (send_sem, recv_sem)
-    barrier_all(ords[0])
+    high, low = rest.pop(0), rest.pop(0)
+    plan, gplan = sketch_plan(rows, grp), gram_plan(rows, grp)
+    parts = []
+    for stages in plan:
+        acc = rest.pop(0)
+        recvs = [rest.pop(0) for _ in stages]
+        parts.append(Halving(stages, acc, recvs, rest.pop(0), rest.pop(0)))
+    grams = []
+    for stages, full in zip(gplan, (full_a, full_b)):
+        acc = rest.pop(0)
+        recvs = [rest.pop(0) for _ in stages]
+        grams.append(Halving(stages, acc, recvs, *[rest.pop(0) for _ in range(2)], full,
+                             *[rest.pop(0) for _ in range(2)]))
+    barrier_all(gplan[0])
     masked, chosen = load_columns(idx_ref, cnt_ref, prior_ref, block_ref)
-    right = split(jnp.concatenate([masked, chosen], axis=1))
-    sk = sketch_ref.shape[0]
+    rh, rl = split(jnp.concatenate([masked, chosen], axis=1))
+    sk, width = sketch_ref.shape[0], rh.shape[1]
     per = sk // n
     step = 512
-    for r in range(0, sk, step):
-        prod = dot3(split(sketch_ref[r:r + step, :]), right)
-        lane = 0
-        for q, w in enumerate(cols):
-            spots = block_at(ords[q], ords[0], n)
-            if q == 0:
-                accs[q][r:r + step, :] = prod[:, lane:lane + w]
-            else:
+    flat = [[g[0] for g in stages] for stages in plan]
+    for lane in range(0, width, 2 * T):
+        wide = min(2 * T, width - lane)
+        for r in range(0, sk, step):
+            if lane == 0:
+                h, l = split(sketch_ref[r:r + step, :])
+                high[r:r + step, :] = h
+                low[r:r + step, :] = l
+            pair = (high[r:r + step, :], low[r:r + step, :])
+            prod = dot3(pair, (rh[:, lane:lane + wide], rl[:, lane:lane + wide]))
+            for j in range(wide // T):
+                q = lane // T + j
+                spots = block_at(flat[q], flat[0], n)
                 for blk in range(r // per, (r + step) // per):
                     s = spots[blk] * per
-                    accs[q][s:s + per, :] = prod[blk * per - r:(blk + 1) * per - r, lane:lane + w]
-            lane += w
-    offs, size = reduce_scatter(
-        [(ords[q], accs[q], recvs[q]) for q in range(len(cols))], sems, 0
-    )
-    mine = jnp.concatenate(
-        [accs[q][pl.ds(pl.multiple_of(offs[q], 8), per)] for q in range(len(cols))], axis=1
-    )
-    gram = dot(mine, mine, 0, 0)
-    width = gram.shape[0] // T
+                    parts[q].acc[s:s + per, :] = prod[blk * per - r:(blk + 1) * per - r, j * T:(j + 1) * T]
+        for j in range(wide // T):
+            parts[lane // T + j].start(0)
+    for i in range(len(plan[0])):
+        for part in parts:
+            part.finish(i)
+            if i + 1 < len(plan[0]):
+                part.start(i + 1)
+    mine = jnp.concatenate([part.acc[rows_at(part.off, per)] for part in parts], axis=1)
     t = 0
-    per_part = 8
-    for i in range(width):
+    for i in range(width // T):
+        strip = dot(mine[:, i * T:(i + 1) * T], mine[:, :(i + 1) * T], 0, 0)
         for j in range(i + 1):
-            q, s = t // per_part, (t % per_part) * T
-            gaccs[q][s:s + T, :] = gram[i * T:(i + 1) * T, j * T:(j + 1) * T]
+            q, s = t // 8, (t % 8) * T
+            grams[q].acc[s:s + T, :] = strip[:, j * T:(j + 1) * T]
             t += 1
+        if t >= 8 and t - i - 1 < 8 and grows == 8 * T:
+            grams[0].start(0)
     for q in range(2):
-        used = min(per_part, t - q * per_part) * T
+        used = min(8, t - q * 8) * T
         if used < grows:
-            gaccs[q][used:grows, :] = jnp.zeros((grows - used, T), F32)
-    parts = [(ords[q], gaccs[q], grecvs[q]) for q in range(2)]
-    offs, size = reduce_scatter(parts, sems, len(cols))
-    for q, full in enumerate((full_a, full_b)):
-        spot = pl.ds(pl.multiple_of(offs[q], 8), size[q])
-        full[spot] = gaccs[q][spot]
-    gather([(ords[0], full_a), (ords[1], full_b)], offs, size, sems, len(cols) + 2)
+            grams[q].acc[used:grows, :] = jnp.zeros((grows - used, T), F32)
+        if q or grows > 8 * T:
+            grams[q].start(0)
+    k = len(gplan[0])
+    for i in range(k):
+        for g in grams:
+            g.finish(i)
+            if i + 1 < k:
+                g.start(i + 1)
+            else:
+                at = rows_at(g.off, g.size)
+                g.full[at] = g.acc[at]
+                g.gstart(k - 1)
+    for i in range(k - 1, -1, -1):
+        for g in grams:
+            g.gfinish()
+            if i:
+                g.gstart(i - 1)
 
 
 def sweep4(tiles, p, inverse):
@@ -298,16 +353,39 @@
     gram_ref[...] = jnp.concatenate([dot(one, one, 0, 0), dot(two, two, 0, 0)], axis=1)
 
 
-def sum_kernel(order, gram_ref, out_ref, hold, recv, send_sem, recv_sem):
-    barrier_all(order)
-    k = len(order)
-    for i, (axis, b) in enumerate(order):
-        src = gram_ref if i == 0 else hold.at[i - 1]
-        c = remote(src, recv.at[i], send_sem.at[i], recv_sem.at[i], axis, b)
-        c.start()
-        c.wait()
-        dst = out_ref if i == k - 1 else hold.at[i]
-        dst[...] = src[...] + recv[i]
+def sum_kernel(rows, grp, gram_ref, out_ref, half, *rest):
+    stages = gram_plan(rows, grp)[0]
+    core, wide = stages[0], stages[1:]
+    slots, holds = rest[:len(wide)], rest[len(wide):2 * len(wide)]
+    send_sem, recv_sem = rest[2 * len(wide):]
+    barrier_all(stages)
+    size = gram_ref.shape[0] // 2
+    mine = rows_at(spot_in(core) * size, size)
+    c = remote(gram_ref.at[rows_at(spot_in(core, 1) * size, size)], half, send_sem.at[0, 0],
+               recv_sem.at[0, 0], core, 1)
+    c.start()
+    c.wait()
+    total = gram_ref[mine, :] + half[...]
+    for i, group in enumerate(wide):
+        src = holds[i]
+        src[...] = total
+        here = spot_in(group)
+        pend = []
+        for m in range(1, 1 << len(group)):
+            c = remote(src, slots[i].at[here], send_sem.at[i + 1, m - 1], recv_sem.at[i + 1, m - 1], group, m)
+            c.start()
+            pend.append(c)
+        slots[i][here] = total
+        for c in pend:
+            c.wait()
+        total = slots[i][0]
+        for m in range(1, 1 << len(group)):
+            total = total + slots[i][m]
+    out_ref[mine, :] = total
+    k = len(stages)
+    c = remote(out_ref.at[mine], out_ref.at[mine], send_sem.at[k, 0], recv_sem.at[k, 0], core, 1)
+    c.start()
+    c.wait()
 
 
 def finish_kernel(scale, gram_ref, resid_ref, x_ref, coef_ref, basis_ref, factors_ref):
@@ -352,22 +430,18 @@
 
 def shards(rows, grp, sketch, prior, block, idx, cnt):
     n = rows * grp
-    n_k = len(orders(rows, grp)[0])
     sk, local = sketch.shape
     width = prior.shape[1]
     vm = pl.BlockSpec(memory_space=pltpu.VMEM)
     sm = pl.BlockSpec(memory_space=pltpu.SMEM)
-    cols = (2 * T, 2 * T, width + T - 4 * T)
     grows = n * max(8, 8 * T // n)
-    scratch = [pltpu.VMEM((sk, w), F32) for w in cols]
-    for w in cols:
-        scratch += [pltpu.VMEM((sk >> (i + 1), w), F32) for i in range(n_k)]
-    scratch += [pltpu.VMEM((grows, T), F32)] * 2
-    for _ in range(2):
-        scratch += [pltpu.VMEM((grows >> (i + 1), T), F32) for i in range(n_k)]
-    scratch += [pltpu.SemaphoreType.DMA((7, n_k))] * 2
+    scratch = [pltpu.VMEM((sk, local), jnp.bfloat16)] * 2
+    for stages in sketch_plan(rows, grp):
+        scratch += [pltpu.VMEM((sk, T), F32)] + recv_shapes(stages, sk, T) + [sem_shape(stages)] * 2
+    for stages in gram_plan(rows, grp):
+        scratch += [pltpu.VMEM((grows, T), F32)] + recv_shapes(stages, grows, T) + [sem_shape(stages)] * 4
     tiles = pl.pallas_call(
-        functools.partial(gram_kernel, rows, grp, n_k, cols, grows),
+        functools.partial(gram_kernel, rows, grp, grows),
         out_shape=[jax.ShapeDtypeStruct((grows, T), F32)] * 2,
         in_specs=[sm, sm, vm, vm, vm],
         out_specs=[vm, vm],
@@ -389,19 +463,19 @@
         scratch_shapes=[pltpu.VMEM((width + T, width + T), F32), pltpu.VMEM((T, T), F32)],
         compiler_params=pltpu.CompilerParams(vmem_limit_bytes=VMEM_LIMIT),
     )(idx, cnt, prior, block, *tiles)
-    order = orders(rows, grp)[0]
     scale = float(local * n) ** 0.5
+    stages = gram_plan(rows, grp)[0]
+    half = P_SIZE // 2
+    most = max((1 << len(g)) - 1 for g in stages)
     gram = pl.pallas_call(
-        functools.partial(sum_kernel, order),
+        functools.partial(sum_kernel, rows, grp),
         out_shape=jax.ShapeDtypeStruct((P_SIZE, T), F32),
         in_specs=[vm],
         out_specs=vm,
-        scratch_shapes=[
-            pltpu.VMEM((n_k, P_SIZE, T), F32),
-            pltpu.VMEM((n_k, P_SIZE, T), F32),
-            pltpu.SemaphoreType.DMA((n_k,)),
-            pltpu.SemaphoreType.DMA((n_k,)),
-        ],
+        scratch_shapes=[pltpu.VMEM((half, T), F32)]
+        + [pltpu.VMEM((1 << len(g), half, T), F32) for g in stages[1:]]
+        + [pltpu.VMEM((half, T), F32) for g in stages[1:]]
+        + [pltpu.SemaphoreType.DMA((len(stages) + 1, most))] * 2,
         compiler_params=pltpu.CompilerParams(collective_id=1, has_side_effects=True),
     )(gram)
     return tuple(pl.pallas_call(

time: 148 us -> 129 us (0.87)
  Pallas kernels: 146 us -> 127 us
    pallas_call x2, Pallas kernels: 96.8 us -> 77.7 us  [the longest x1 65.3 us: shards(): pl.pallas_call(functools.partial(gram_kernel, rows, grp, grows), out_shap...]
where the time goes in v3:
time: 129 us; the launch traced here: 128 us
  Pallas kernels  127 us (98%)
  between operations  1.94 us (2%)
    pallas_call x1, Pallas kernels, shards(): pl.pallas_call(functools.partial(gram_kernel, rows, grp, grows), out_shap...  65.3 us
    pallas_call x1, Pallas kernels, shards(): pl.pallas_call(solve_kernel, out_shape=[jax.ShapeDtypeStruct((width, T),...  40.6 us
    pallas_call x1, Pallas kernels, shards(): pl.pallas_call(functools.partial(sum_kernel, rows, grp), out_shape=jax.Sh...  12.4 us
    pallas_call x1, Pallas kernels, shards(): pl.pallas_call(functools.partial(finish_kernel, scale), out_shape=[jax.Sh...  8.24 us

profile of v3, /device:TPU:0, one launch (start us, length us, event | category | flops | bytes accessed | tf_op | source)
XLA Modules:
  0.0 128.5 jit_solution(15167861331828178936)
XLA Ops:
  1.9 65.3 %shard_map.68 = (f32[1024,128]{1,0:T(8,128)}, f32[1024,128]{1,0:T(8,128)}) custom-call(s32[1]{0:T(128)S(6)} %copy.7.idx_ref, s32[1]{0:T(128)S(6)} %copy.8.cnt_ref, f32[2048,256]{1,0:T(8,128)} %sketch_ref.1, f32[256,512]{1,0:T(8,128)} %prior_ref.3, f32[256,256]{1,0:T(8,128)} %block_ref.3), custom_call_target="tpu_custom_call" | custom-call | tf_op jit(solution)/shard_map/pallas_call | solution.py:443
  67.2 40.6 %shard_map.69 = (f32[512,128]{1,0:T(8,128)}, f32[64,64]{1,0:T(8,128)}, f32[256,128]{1,0:T(8,128)}, f32[64,128]{1,0:T(8,128)}) custom-call(s32[1]{0:T(128)S(6)} %copy.7.idx_ref, s32[1]{0:T(128)S(6)} %copy.8.cnt_ref, f32[256,512]{1,0:T(8,128)} %prior_ref.3, f32[256,256]{1,0:T(8,128)} %block_ref.3, f32[1024,128]{1,0:T(8,128)} %get-tuple-element.8.ta_ref, ...), custom_call_target="tpu_custom_call" | custom-call | tf_op jit(solution)/shard_map/pallas_call | solution.py:453
  107.8 12.4 %shard_map.70.gram_ref = f32[64,128]{1,0:T(8,128)} custom-call(f32[64,128]{1,0:T(8,128)} %get-tuple-element.10.gram_ref), custom_call_target="tpu_custom_call" | custom-call | tf_op jit(solution)/shard_map/pallas_call | solution.py:470
  120.2 8.2 %shard_map.71 = (f32[256,128]{1,0:T(8,128)}, f32[640,128]{1,0:T(8,128)}) custom-call(f32[64,128]{1,0:T(8,128)} %shard_map.70.gram_ref, f32[256,128]{1,0:T(8,128)} %get-tuple-element.11.resid_ref, f32[64,64]{1,0:T(8,128)} %get-tuple-element.12.x_ref, f32[512,128]{1,0:T(8,128)} %get-tuple-element.13.coef_ref), custom_call_target="tpu_custom_call" | custom-call | tf_op jit(solution)/shard_map/pallas_call | solution.py:481

commit v4 on v3

--- a/solution.py
+++ b/solution.py
@@ -260,14 +260,16 @@
                 g.gstart(i - 1)
 
 
-def sweep4(tiles, p, inverse):
-    v, o = p // 8, p % 8
-    lane = lax.broadcasted_iota(jnp.int32, (8, T), 1)
-    sub = lax.broadcasted_iota(jnp.int32, (8, T), 0)
-    r = [jnp.broadcast_to(tiles[v][o + i:o + i + 1, :], (8, T)) for i in range(4)]
+def solve4(tile, p, sides):
+    o = p % 8
+
+    def spread(t):
+        return [jnp.broadcast_to(t[o + i:o + i + 1, :], (8, T)) for i in range(4)]
+
+    own = spread(tile)
 
     def at(i, j):
-        return jnp.broadcast_to(r[i][:, p + j:p + j + 1], (8, T))
+        return jnp.broadcast_to(own[i][:, p + j:p + j + 1], (8, T))
 
     a, b, e, f = at(0, 0), at(0, 1), at(0, 2), at(0, 3)
     c, g, h = at(1, 1), at(1, 2), at(1, 3)
@@ -279,24 +281,50 @@
     s01 = y - (e * k01 + g * k11)
     s11 = z - (f * k01 + h * k11)
     rs = 1.0 / (s00 * s11 - s01 * s01)
-    inside = (lane >= p) & (lane < p + 4)
-    if inverse:
-        r = [jnp.where(inside, jnp.where(lane == p + i, 1.0, 0.0), r[i]) for i in range(4)]
-    g0, g1 = (c * r[0] - b * r[1]) * ra, (a * r[1] - b * r[0]) * ra
-    q2 = r[2] - (k00 * r[0] + k10 * r[1])
-    q3 = r[3] - (k01 * r[0] + k11 * r[1])
-    n2, n3 = (s11 * q2 - s01 * q3) * rs, (s00 * q3 - s01 * q2) * rs
-    n0, n1 = g0 - (k00 * n2 + k01 * n3), g1 - (k10 * n2 + k11 * n3)
+    out = []
+    for side in sides:
+        r = spread(side)
+        g0, g1 = (c * r[0] - b * r[1]) * ra, (a * r[1] - b * r[0]) * ra
+        q2 = r[2] - (k00 * r[0] + k10 * r[1])
+        q3 = r[3] - (k01 * r[0] + k11 * r[1])
+        n2, n3 = (s11 * q2 - s01 * q3) * rs, (s00 * q3 - s01 * q2) * rs
+        out.append([g0 - (k00 * n2 + k01 * n3), g1 - (k10 * n2 + k11 * n3), n2, n3])
+    return out
+
+
+def put4(tile, p, rows):
+    sub = lax.broadcasted_iota(jnp.int32, (8, T), 0)
+    for j, row in enumerate(rows):
+        tile = jnp.where(sub == p % 8 + j, row, tile)
+    return tile
+
+
+def eliminate4(tiles, p):
+    v = p // 8
+    rows, = solve4(tiles[v], p, [tiles[v]])
     new = []
-    for u, tile in enumerate(tiles):
-        w = jnp.where(inside, 0.0, tile) if inverse else tile
-        for j, row in enumerate((n0, n1, n2, n3)):
-            w = w - tile[:, p + j:p + j + 1] * row
+    for u, w in enumerate(tiles):
+        tile = w
+        for j in range(4):
+            w = w - tile[:, p + j:p + j + 1] * rows[j]
+        new.append(put4(w, p, rows) if u == v else w)
+    return new
+
+
+def factor4(mat, low, norm, p):
+    v, o = p // 8, p % 8
+    sub = lax.broadcasted_iota(jnp.int32, (8, T), 0)
+    rows, lows = solve4(mat[v], p, [mat[v], low[v]])
+    norm[v] = put4(norm[v], p, lows)
+    for u in range(v if o == 0 else v + 1, len(mat)):
+        w, l = mat[u], low[u]
+        for j in range(4):
+            col = jnp.broadcast_to(mat[u][:, p + j:p + j + 1], (8, T))
+            w = w - col * rows[j]
+            l = l - col * lows[j]
         if u == v:
-            for j, row in enumerate((n0, n1, n2, n3)):
-                w = jnp.where(sub == o + j, row, w)
-        new.append(w)
-    return new
+            w, l = jnp.where(sub >= 4, w, mat[u]), jnp.where(sub >= 4, l, low[u])
+        mat[u], low[u] = w, l
 
 
 def solve_kernel(idx_ref, cnt_ref, prior_ref, block_ref, ta_ref, tb_ref,
@@ -320,10 +348,14 @@
     def body(k, _):
         at = pl.ds(pl.multiple_of(k * T, T), T)
         d = a_ref[at, at]
-        tiles = [d[8 * v:8 * v + 8, :] for v in range(T // 8)]
+        mat = [d[8 * v:8 * v + 8, :] for v in range(T // 8)]
+        lane = lax.broadcasted_iota(jnp.int32, (8, T), 1)
+        sub = lax.broadcasted_iota(jnp.int32, (8, T), 0)
+        low = [jnp.where(lane == sub + 8 * v, 1.0, 0.0) for v in range(T // 8)]
+        norm = [jnp.zeros((8, T), F32) for v in range(T // 8)]
         for p in range(0, T, 4):
-            tiles = sweep4(tiles, p, True)
-        inv_ref[...] = jnp.concatenate(tiles, axis=0)
+            factor4(mat, low, norm, p)
+        inv_ref[...] = dot(jnp.concatenate(low, axis=0), jnp.concatenate(norm, axis=0), 0, 0)
         for kk in range(blocks - 1):
             @pl.when(k == kk)
             def _():
@@ -342,7 +374,7 @@
     e = a_ref[width:width + P_SIZE, width:width + T]
     tiles = [e[8 * v:8 * v + 8, :] for v in range(P_SIZE // 8)]
     for p in range(0, P_SIZE, 4):
-        tiles = sweep4(tiles, p, False)
+        tiles = eliminate4(tiles, p)
     x = jnp.concatenate(tiles, axis=0)[:, P_SIZE:]
     x_ref[...] = x
     masked, chosen = load_columns(idx_ref, cnt_ref, prior_ref, block_ref)

time: 129 us -> 123 us (0.953)
  Pallas kernels: 127 us -> 120 us
    pallas_call x1, Pallas kernels: 40.6 us -> 34.4 us  [shards(): pl.pallas_call(solve_kernel, out_shape=[jax.ShapeDtypeStruct((width, T),...]
where the time goes in v4:
time: 123 us; the launch traced here: 122 us
  Pallas kernels  120 us (98%)
  between operations  1.94 us (2%)
    pallas_call x1, Pallas kernels, shards(): pl.pallas_call(functools.partial(gram_kernel, rows, grp, grows), out_shap...  65.3 us
    pallas_call x1, Pallas kernels, shards(): pl.pallas_call(solve_kernel, out_shape=[jax.ShapeDtypeStruct((width, T),...  34.4 us
    pallas_call x1, Pallas kernels, shards(): pl.pallas_call(functools.partial(sum_kernel, rows, grp), out_shape=jax.Sh...  12.4 us
    pallas_call x1, Pallas kernels, shards(): pl.pallas_call(functools.partial(finish_kernel, scale), out_shape=[jax.Sh...  8.24 us

profile of v4, /device:TPU:0, one launch (start us, length us, event | category | flops | bytes accessed | tf_op | source)
XLA Modules:
  0.0 122.2 jit_solution(973937934127870342)
XLA Ops:
  1.9 65.3 %shard_map.68 = (f32[1024,128]{1,0:T(8,128)}, f32[1024,128]{1,0:T(8,128)}) custom-call(s32[1]{0:T(128)S(6)} %copy.7.idx_ref, s32[1]{0:T(128)S(6)} %copy.8.cnt_ref, f32[2048,256]{1,0:T(8,128)} %sketch_ref.1, f32[256,512]{1,0:T(8,128)} %prior_ref.3, f32[256,256]{1,0:T(8,128)} %block_ref.3), custom_call_target="tpu_custom_call" | custom-call | tf_op jit(solution)/shard_map/pallas_call | solution.py:475
  67.2 34.4 %shard_map.69 = (f32[512,128]{1,0:T(8,128)}, f32[64,64]{1,0:T(8,128)}, f32[256,128]{1,0:T(8,128)}, f32[64,128]{1,0:T(8,128)}) custom-call(s32[1]{0:T(128)S(6)} %copy.7.idx_ref, s32[1]{0:T(128)S(6)} %copy.8.cnt_ref, f32[256,512]{1,0:T(8,128)} %prior_ref.3, f32[256,256]{1,0:T(8,128)} %block_ref.3, f32[1024,128]{1,0:T(8,128)} %get-tuple-element.8.ta_ref, ...), custom_call_target="tpu_custom_call" | custom-call | tf_op jit(solution)/shard_map/pallas_call | solution.py:485
  101.6 12.4 %shard_map.70.gram_ref = f32[64,128]{1,0:T(8,128)} custom-call(f32[64,128]{1,0:T(8,128)} %get-tuple-element.10.gram_ref), custom_call_target="tpu_custom_call" | custom-call | tf_op jit(solution)/shard_map/pallas_call | solution.py:502
  114.0 8.2 %shard_map.71 = (f32[256,128]{1,0:T(8,128)}, f32[640,128]{1,0:T(8,128)}) custom-call(f32[64,128]{1,0:T(8,128)} %shard_map.70.gram_ref, f32[256,128]{1,0:T(8,128)} %get-tuple-element.11.resid_ref, f32[64,64]{1,0:T(8,128)} %get-tuple-element.12.x_ref, f32[512,128]{1,0:T(8,128)} %get-tuple-element.13.coef_ref), custom_call_target="tpu_custom_call" | custom-call | tf_op jit(solution)/shard_map/pallas_call | solution.py:513

commit v5 on v4

--- a/solution.py
+++ b/solution.py
@@ -158,7 +158,7 @@
 
 def gram_plan(rows, grp):
     core, y, x, z = axes_of(rows, grp)
-    return [[g for g in (core, x + y, z) if g], [g for g in (core, z, x + y) if g]]
+    return [[g for g in (core, x + y, z) if g], [g for g in (core, x + y, z) if g]]
 
 
 def block_at(order, target, n):
@@ -429,20 +429,29 @@
     for h in range(2):
         m = jnp.concatenate([gram[:, h * P_SIZE:(h + 1) * P_SIZE], eye], axis=1)
         mats.append([m[8 * v:8 * v + 8, :] for v in range(P_SIZE // 8)])
-    for p in range(P_SIZE):
+    for p in range(0, P_SIZE, 2):
         v, o = p // 8, p % 8
         for h in range(2):
             tiles = mats[h]
-            row = tiles[v][o:o + 1, :]
-            d = row[:, p:p + 1]
-            y = lax.rsqrt(d)
-            y = y * (1.5 - 0.5 * d * y * y)
-            row = row * y
+            r0, r1 = (jnp.broadcast_to(tiles[v][o + i:o + i + 1, :], (8, T)) for i in range(2))
+            a, b = (jnp.broadcast_to(r0[:, p + i:p + i + 1], (8, T)) for i in range(2))
+            c = jnp.broadcast_to(r1[:, p + 1:p + 2], (8, T))
+            y0 = lax.rsqrt(a)
+            y0 = y0 * (1.5 - 0.5 * a * y0 * y0)
+            side = b * y0
+            d = c - side * side
+            y1 = lax.rsqrt(d)
+            y1 = y1 * (1.5 - 0.5 * d * y1 * y1)
+            row0 = r0 * y0
+            row1 = (r1 - side * row0) * y1
             new = list(tiles)
             for u in range(v, P_SIZE // 8):
-                w = tiles[u] - (tiles[u][:, p:p + 1] * y) * row
+                c0 = tiles[u][:, p:p + 1] * y0
+                c1 = (tiles[u][:, p + 1:p + 2] - c0 * side) * y1
+                w = tiles[u] - c0 * row0 - c1 * row1
                 if u == v:
-                    w = jnp.where(sub == o, row, jnp.where(sub > o, w, tiles[u]))
+                    w = jnp.where(sub > o + 1, w, tiles[u])
+                    w = jnp.where(sub == o, row0, jnp.where(sub == o + 1, row1, w))
                 new[u] = w
             mats[h] = new
     full = [jnp.concatenate(m, axis=0) for m in mats]

time: 123 us -> 122 us (level)
  no operation moved by 1% of the time
where the time goes in v5:
time: 122 us; the launch traced here: 121 us
  Pallas kernels  119 us (98%)
  between operations  1.94 us (2%)
    pallas_call x1, Pallas kernels, shards(): pl.pallas_call(functools.partial(gram_kernel, rows, grp, grows), out_shap...  65.2 us
    pallas_call x1, Pallas kernels, shards(): pl.pallas_call(solve_kernel, out_shape=[jax.ShapeDtypeStruct((width, T),...  34.4 us
    pallas_call x1, Pallas kernels, shards(): pl.pallas_call(functools.partial(sum_kernel, rows, grp), out_shape=jax.Sh...  12.4 us
    pallas_call x1, Pallas kernels, shards(): pl.pallas_call(functools.partial(finish_kernel, scale), out_shape=[jax.Sh...  7.46 us

profile of v5, /device:TPU:0, one launch (start us, length us, event | category | flops | bytes accessed | tf_op | source)
XLA Modules:
  0.0 121.4 jit_solution(8871948224252758805)
XLA Ops:
  1.9 65.2 %shard_map.68 = (f32[1024,128]{1,0:T(8,128)}, f32[1024,128]{1,0:T(8,128)}) custom-call(s32[1]{0:T(128)S(6)} %copy.7.idx_ref, s32[1]{0:T(128)S(6)} %copy.8.cnt_ref, f32[2048,256]{1,0:T(8,128)} %sketch_ref.1, f32[256,512]{1,0:T(8,128)} %prior_ref.3, f32[256,256]{1,0:T(8,128)} %block_ref.3), custom_call_target="tpu_custom_call" | custom-call | tf_op jit(solution)/shard_map/pallas_call | solution.py:484
  67.2 34.4 %shard_map.69 = (f32[512,128]{1,0:T(8,128)}, f32[64,64]{1,0:T(8,128)}, f32[256,128]{1,0:T(8,128)}, f32[64,128]{1,0:T(8,128)}) custom-call(s32[1]{0:T(128)S(6)} %copy.7.idx_ref, s32[1]{0:T(128)S(6)} %copy.8.cnt_ref, f32[256,512]{1,0:T(8,128)} %prior_ref.3, f32[256,256]{1,0:T(8,128)} %block_ref.3, f32[1024,128]{1,0:T(8,128)} %get-tuple-element.8.ta_ref, ...), custom_call_target="tpu_custom_call" | custom-call | tf_op jit(solution)/shard_map/pallas_call | solution.py:494
  101.6 12.4 %shard_map.70.gram_ref = f32[64,128]{1,0:T(8,128)} custom-call(f32[64,128]{1,0:T(8,128)} %get-tuple-element.10.gram_ref), custom_call_target="tpu_custom_call" | custom-call | tf_op jit(solution)/shard_map/pallas_call | solution.py:511
  113.9 7.5 %shard_map.71 = (f32[256,128]{1,0:T(8,128)}, f32[640,128]{1,0:T(8,128)}) custom-call(f32[64,128]{1,0:T(8,128)} %shard_map.70.gram_ref, f32[256,128]{1,0:T(8,128)} %get-tuple-element.11.resid_ref, f32[64,64]{1,0:T(8,128)} %get-tuple-element.12.x_ref, f32[512,128]{1,0:T(8,128)} %get-tuple-element.13.coef_ref), custom_call_target="tpu_custom_call" | custom-call | tf_op jit(solution)/shard_map/pallas_call | solution.py:522
